TPU v7x, 32 devices: a whole 2x2x4 slice. The times are simulated.
32 devices in a mesh: wide: 4 (over y, x), narrow: 8 (over z, core).
Axes of the slice: x: 2, y: 2, z: 4, core: 2. Of those that a mesh axis runs over, the one named last changes fastest.
Arguments:
- mixture: bfloat16 [4, 64, 256, 256], P(None, ('wide', 'narrow')), may hold values from -30 to 30
- w_attn: bfloat16 [2, 4, 256, 256], replicated, may hold values from -2.625 to 2.625
- w_up: bfloat16 [2, 256, 1024], replicated, may hold values from -0.375 to 0.375
- w_down: bfloat16 [2, 1024, 256], replicated, may hold values from -0.1875 to 0.1875
- norm_gain: float32 [2, 2, 256], replicated, may hold values from 0.1 to 1.9
- norm_bias: float32 [2, 2, 256], replicated, may hold values from -3 to 3
- group_gain: float32 [2, 256], replicated, may hold values from 0.1 to 1.9
- group_bias: float32 [2, 256], replicated, may hold values from -3 to 3
Outputs:
- separated: bfloat16 [4, 64, 256, 256], P(None, ('wide', 'narrow'))
All inputs are finite; a program needn't handle non-finite values.
Results may differ from a plain program's by a relative error of at most 0.0083.
Values may be sent and summed in bfloat16 or wider, within the bound.
A program may use at most 64 MiB of HBM per device.

v0:
```python
import math
import jax
import jax.numpy as jnp
from jax import lax
from jax.sharding import PartitionSpec as P

HEADS = 8
EPSILON = 1e-05


def positions_table(seq_length, model_width):
    positions = jnp.arange(seq_length, dtype=jnp.float32)[:, None]
    freq_index = jnp.arange(model_width // 2, dtype=jnp.float32)[None, :]
    angles = positions * jnp.exp(freq_index * (-2.0 * math.log(10000.0) / model_width))
    return jnp.concatenate([jnp.sin(angles), jnp.cos(angles)], axis=1)


def layer_norm(values, gain_row, bias_row):
    mean_value = jnp.mean(values, axis=-1, keepdims=True)
    centered = values - mean_value
    variance = jnp.mean(centered * centered, axis=-1, keepdims=True)
    return centered * lax.rsqrt(variance + EPSILON) * gain_row + bias_row


def encoder_block(seq_block, pos_table, attn_weights, up_weight, down_weight, gains, biases):
    groups, seq_length, inner_count, model_width = seq_block.shape
    head_size = model_width // HEADS
    state_rows = seq_block.astype(jnp.float32) + pos_table[None, :, None, :]
    normed = (
        layer_norm(state_rows, gains[0], biases[0]).astype(jnp.bfloat16).reshape(-1, model_width)
    )

    def project(matrix):
        product = jnp.dot(normed, matrix, preferred_element_type=jnp.float32).astype(jnp.bfloat16)
        return product.reshape(groups, seq_length, inner_count, HEADS, head_size)

    queries = project(attn_weights[0])
    key_rows = project(attn_weights[1])
    value_rows = project(attn_weights[2])
    scores = jnp.einsum("alnhe,amnhe->anhlm", queries, key_rows, preferred_element_type=jnp.float32)
    scores = scores * (1.0 / math.sqrt(head_size))
    shifted = jnp.exp(scores - jnp.max(scores, axis=-1, keepdims=True))
    weights = (shifted / jnp.sum(shifted, axis=-1, keepdims=True)).astype(jnp.bfloat16)
    attended = jnp.einsum(
        "anhlm,amnhe->alnhe", weights, value_rows, preferred_element_type=jnp.float32
    )
    attended = attended.astype(jnp.bfloat16).reshape(-1, model_width)
    mixed = jnp.dot(attended, attn_weights[3], preferred_element_type=jnp.float32)
    state_after = state_rows + mixed.reshape(state_rows.shape)
    normed_two = (
        layer_norm(state_after, gains[1], biases[1]).astype(jnp.bfloat16).reshape(-1, model_width)
    )
    hidden = jax.nn.relu(jnp.dot(normed_two, up_weight, preferred_element_type=jnp.float32)).astype(
        jnp.bfloat16
    )
    output = jnp.dot(hidden, down_weight, preferred_element_type=jnp.float32)
    return state_after + output.reshape(state_after.shape)


def run_layer(seq_data, layer_index, w_attn, w_up, w_down, norm_gain, norm_bias, block_rows):
    seq_count, seq_length, inner_count, model_width = seq_data.shape
    per_block = math.gcd(seq_count, max(1, block_rows // (seq_length * inner_count)))
    pos_table = positions_table(seq_length, model_width)
    blocked = seq_data.reshape(
        seq_count // per_block, per_block, seq_length, inner_count, model_width
    )

    def apply_block(seq_block):
        return encoder_block(
            seq_block,
            pos_table,
            w_attn[layer_index],
            w_up[layer_index],
            w_down[layer_index],
            norm_gain[layer_index],
            norm_bias[layer_index],
        )

    return lax.map(apply_block, blocked).reshape(seq_count, seq_length, inner_count, model_width)


def group_norm(values, gain_row, bias_row):
    cell_count = (
        values.shape[1] * lax.axis_size(("wide", "narrow")) * values.shape[2] * values.shape[3]
    )
    totals, squares = lax.psum(
        (jnp.sum(values, axis=(1, 2, 3)), jnp.sum(values * values, axis=(1, 2, 3))),
        ("wide", "narrow"),
    )
    mean_flat = totals / cell_count
    variance = squares / cell_count - mean_flat * mean_flat
    centered = values - mean_flat[:, None, None, None]
    return centered * lax.rsqrt(variance[:, None, None, None] + EPSILON) * gain_row + bias_row


def on_device(mixture, w_attn, w_up, w_down, norm_gain, norm_bias, group_gain, group_bias):
    mix_count, segs_here, frame_count, model_width = mixture.shape
    intra_out = run_layer(
        mixture.reshape(mix_count * segs_here, frame_count, 1, model_width),
        0,
        w_attn,
        w_up,
        w_down,
        norm_gain,
        norm_bias,
        512,
    ).reshape(mixture.shape)
    carried = (
        group_norm(intra_out, group_gain[0], group_bias[0]) + mixture.astype(jnp.float32)
    ).astype(jnp.bfloat16)
    result = run_layer(
        lax.all_to_all(carried, ("wide", "narrow"), split_axis=2, concat_axis=1, tiled=True),
        1,
        w_attn,
        w_up,
        w_down,
        norm_gain,
        norm_bias,
        512,
    ).astype(jnp.bfloat16)
    inter_out = lax.all_to_all(result, ("wide", "narrow"), split_axis=1, concat_axis=2, tiled=True)
    separated = group_norm(
        inter_out.astype(jnp.float32), group_gain[1], group_bias[1]
    ) + carried.astype(jnp.float32)
    return separated.astype(jnp.bfloat16)


def solution(mesh):
    in_specs = (P(None, ("wide", "narrow"), None, None), P(), P(), P(), P(), P(), P(), P())
    out_specs = P(None, ("wide", "narrow"), None, None)
    return jax.shard_map(
        on_device, mesh=mesh, in_specs=in_specs, out_specs=out_specs, check_vma=False
    )
```

profile of v0, /device:TPU:10, one launch (start us, length us, event | category | flops | bytes accessed | tf_op | source)
XLA Modules:
  0.0 288.5 jit_solution(8594341458941040517)
XLA Ops:
  0.6 69.5 %while.20 = (s32[]{:T(128)}, f32[4,2,256,1,256]{4,2,1,3,0:T(8,128)S(1)}, bf16[4,2,256,1,256]{4,2,1,3,0:T(8,128)(2,1)}, f32[256,256]{1,0:T(8,128)S(1)}, f32[2,2,2...) while((s32[]{:T(128)}, ...), condition=%wide.region_7.8_spmd, body=%wide.region_0.7_spmd.sunk | while | flops 950011136 | bytes 32064172 | solution.py:79
  7.5 3.5 %fusion.222 = (f32[2,8,256]{2,1,0:T(8,128)S(1)}, f32[2,8,256,256]{2,3,1,0:T(8,128)}) fusion(bf16[2,256,8,32]{1,0,3,2:T(2,128)(2,1)S(1)} %reshape.950, bf16[2,256,8,32]{1,0,3,2:T(2,128)(2,1)S(1)} %reshape.951), kind=kOutput, calls=%fused_computation.148.clone.1 | convolution fusion | flops 70254848 | bytes 4734976 | tf_op jit(solution)/shard_map/while/body/eval_jaxpr/sub | solution.py:42
  12.4 2.6 fusion.223
  24.9 3.4 %fusion.222 = (f32[2,8,256]{2,1,0:T(8,128)S(1)}, f32[2,8,256,256]{2,3,1,0:T(8,128)}) fusion(bf16[2,256,8,32]{1,0,3,2:T(2,128)(2,1)S(1)} %reshape.950, bf16[2,256,8,32]{1,0,3,2:T(2,128)(2,1)S(1)} %reshape.951), kind=kOutput, calls=%fused_computation.148.clone.1 | convolution fusion | flops 70254848 | bytes 4734976 | tf_op jit(solution)/shard_map/while/body/eval_jaxpr/sub | solution.py:42
  29.7 2.6 fusion.223
  42.3 3.4 %fusion.222 = (f32[2,8,256]{2,1,0:T(8,128)S(1)}, f32[2,8,256,256]{2,3,1,0:T(8,128)}) fusion(bf16[2,256,8,32]{1,0,3,2:T(2,128)(2,1)S(1)} %reshape.950, bf16[2,256,8,32]{1,0,3,2:T(2,128)(2,1)S(1)} %reshape.951), kind=kOutput, calls=%fused_computation.148.clone.1 | convolution fusion | flops 70254848 | bytes 4734976 | tf_op jit(solution)/shard_map/while/body/eval_jaxpr/sub | solution.py:42
  47.1 2.6 fusion.223
  59.7 3.4 %fusion.222 = (f32[2,8,256]{2,1,0:T(8,128)S(1)}, f32[2,8,256,256]{2,3,1,0:T(8,128)}) fusion(bf16[2,256,8,32]{1,0,3,2:T(2,128)(2,1)S(1)} %reshape.950, bf16[2,256,8,32]{1,0,3,2:T(2,128)(2,1)S(1)} %reshape.951), kind=kOutput, calls=%fused_computation.148.clone.1 | convolution fusion | flops 70254848 | bytes 4734976 | tf_op jit(solution)/shard_map/while/body/eval_jaxpr/sub | solution.py:42
  64.5 2.6 fusion.223
  71.9 41.2 %all-reduce.1 = (f32[4]{0:T(128)S(1)}, f32[4]{0:T(128)S(1)}) all-reduce(f32[4]{0:T(128)S(1)} %fusion.124, f32[4]{0:T(128)S(1)} %reduce_sum.126), channel_id=1, replica_groups=mesh['wide'=4,'narrow'=8] {'wide','narrow'}, use_global_device_ids=true, to_apply=%region_11.12 | all-reduce | flops 8 | bytes 64 | tf_op jit(solution)/shard_map/psum | solution.py:86
  114.5 1.8 copy.87
  116.3 3.9 %all-to-all-start = ((bf16[4,2,256,256]{3,0,1,2:T(4,128)(2,1)}), bf16[4,2,256,256]{3,0,1,2:T(4,128)(2,1)S(1)}, u32[]{:S(2)}, u32[]{:S(2)}) async-start(bf16[4,2,256,256]{3,0,1,2:T(4,128)(2,1)} %copy.87), calls=%async_computation | async-start | bytes 2097152 | tf_op jit(solution)/shard_map/all_to_all | solution.py:112
  120.4 24.5 %all-to-all-done = bf16[4,2,256,256]{3,0,1,2:T(4,128)(2,1)S(1)} async-done(((bf16[4,2,256,256]{3,0,1,2:T(4,128)(2,1)}), bf16[4,2,256,256]{3,0,1,2:T(4,128)(2,1)S(1)}, u32[]{:S(2)}, u32[]{:S(2)}) %all-to-all-start) | async-done | bytes 1048608 | tf_op jit(solution)/shard_map/all_to_all | solution.py:112
  145.1 69.6 %while.21 = (s32[]{:T(128)}, bf16[4,1,64,8,256]{4,3,0,2,1:T(8,128)(2,1)}, bf16[4,1,64,8,256]{4,3,2,1,0:T(8,128)(2,1)S(1)}, f32[64,256]{1,0:T(8,128)S(1)}, f32[2,...) while((s32[]{:T(128)}, ...), condition=%wide.region_19.20_spmd, body=%wide.region_12.19_spmd.sunk | while | flops 864556160 | bytes 17468152 | solution.py:79
  148.9 2.7 fusion.246
  151.6 2.0 fusion.245
  155.3 2.7 convolution_convert_fusion.20
  159.8 2.6 fusion.248
  166.3 2.7 fusion.246
  169.0 2.0 fusion.245
  172.7 2.7 convolution_convert_fusion.20
  177.2 2.6 fusion.248
  183.7 2.7 fusion.246
  186.4 2.0 fusion.245
  190.1 2.7 convolution_convert_fusion.20
  194.6 2.6 fusion.248
  201.1 2.7 fusion.246
  203.8 2.0 fusion.245
  207.5 2.7 convolution_convert_fusion.20
  212.0 2.6 fusion.248
  214.7 30.2 %all_to_all.24 = bf16[4,64,8,256]{3,2,0,1:T(8,128)(2,1)S(1)} all-to-all(bf16[4,64,8,256]{3,2,0,1:T(8,128)(2,1)} %bitcast.314), channel_id=1, replica_groups=mesh['wide'=4,'narrow'=8] {'wide','narrow'}, dimensions={1} | all-to-all | bytes 2097152 | tf_op jit(solution)/shard_map/all_to_all | solution.py:121
  245.4 41.5 %all-reduce = (f32[4]{0:T(128)S(1)}, f32[4]{0:T(128)S(1)}) all-reduce(f32[4]{0:T(128)S(1)} %get-tuple-element.102, f32[4]{0:T(128)S(1)} %get-tuple-element.101), channel_id=1, replica_groups=mesh['wide'=4,'narrow'=8] {'wide','narrow'}, use_global_device_ids=true, to_apply=%region_23.24 | all-reduce | flops 8 | bytes 64 | tf_op jit(solution)/shard_map/psum | solution.py:86
  (243 shorter events, 79.5 us)
Async XLA Ops:
  15.0 2.1 copy-start.15
  15.0 2.5 copy-start.3
  32.3 2.1 copy-start.15
  32.4 2.5 copy-start.3
  49.7 2.1 copy-start.15
  49.7 2.5 copy-start.3
  67.1 2.1 copy-start.15
  67.1 2.5 copy-start.3
  70.1 43.0 %copy-start = (bf16[4,2,256,1,256]{4,2,1,3,0:T(8,128)(2,1)S(1)}, bf16[4,2,256,1,256]{4,2,1,3,0:T(8,128)(2,1)}, u32[]{:S(2)}) copy-start(bf16[4,2,256,1,256]{4,2,1,3,0:T(8,128)(2,1)} %get-tuple-element.371) | copy-start | bytes 3145732
  116.3 28.7 %copy-start.5 = (f32[2,2,256]{2,1,0:T(2,128)S(1)}, f32[2,2,256]{2,1,0:T(2,128)}, u32[]{:S(2)}) copy-start(f32[2,2,256]{2,1,0:T(2,128)} %get-tuple-element.375) | copy-start | bytes 12292
  116.3 28.7 %copy-start.6 = (f32[2,2,256]{2,1,0:T(2,128)S(1)}, f32[2,2,256]{2,1,0:T(2,128)}, u32[]{:S(2)}) copy-start(f32[2,2,256]{2,1,0:T(2,128)} %get-tuple-element.376) | copy-start | bytes 12292
  116.3 28.5 %all-to-all-start = ((bf16[4,2,256,256]{3,0,1,2:T(4,128)(2,1)}), bf16[4,2,256,256]{3,0,1,2:T(4,128)(2,1)S(1)}, u32[]{:S(2)}, u32[]{:S(2)}) async-start(bf16[4,2,256,256]{3,0,1,2:T(4,128)(2,1)} %copy.87), calls=%async_computation | async-start | bytes 2097152 | tf_op jit(solution)/shard_map/all_to_all | solution.py:112
  145.5 1.7 copy-start.7
  151.6 2.0 copy-start.8
  151.6 2.0 copy-start.10
  158.0 1.8 copy-start.4
  162.9 1.7 copy-start.7
  162.9 1.7 copy-start.9
  169.0 2.0 copy-start.8
  169.0 2.0 copy-start.10
  175.4 1.8 copy-start.4
  186.4 2.0 copy-start.8
  186.4 2.0 copy-start.10
  192.8 1.8 copy-start.4
  197.7 1.7 copy-start.7
  197.7 1.7 copy-start.9
  203.8 2.0 copy-start.8
  203.8 2.0 copy-start.10
  210.2 1.8 copy-start.4
  214.7 72.2 %copy-start.2 = (bf16[4,2,256,256]{3,2,1,0:T(8,128)(2,1)S(1)}, bf16[4,2,256,256]{3,2,1,0:T(8,128)(2,1)}, u32[]{:S(2)}) copy-start(bf16[4,2,256,256]{3,2,1,0:T(8,128)(2,1)} %copy-done.1) | copy-start | bytes 3145732
  214.7 72.2 %copy-start.11 = (f32[1,256]{1,0:T(1,128)S(1)}, f32[1,256]{1,0:T(1,128)}, u32[]{:S(2)}) copy-start(f32[1,256]{1,0:T(1,128)} %get-tuple-element.161) | copy-start | bytes 3076
  214.7 72.2 %copy-start.12 = (f32[1,256]{1,0:T(1,128)S(1)}, f32[1,256]{1,0:T(1,128)}, u32[]{:S(2)}) copy-start(f32[1,256]{1,0:T(1,128)} %get-tuple-element.163) | copy-start | bytes 3076
  (6 other events, 8.0 us)
where the time goes:
time: 290 us; the launch traced here: 288 us
  blocking collectives  113 us (39%)
  matrix products  107 us (37%)
  waiting for transfers between devices  24.5 us (8%)
  other arithmetic  22.1 us (8%)
  local copies, waits for them, and re-layouts  16.2 us (6%)
  starting transfers between devices  3.87 us (1%)
    psum x2, blocking collectives, group_norm(): lax.psum((jnp.sum(values, axis=(1, 2, 3)), jnp.sum(values * values, axis=...  82.7 us
    all_to_all x1, blocking collectives, on_device(): lax.all_to_all(result, ('wide', 'narrow'), split_axis=1, concat_axis=2, t...  30.2 us
    dot_general x24, matrix products, project(): jnp.dot(normed, matrix, preferred_element_type=jnp.float32)  28.3 us
    all_to_all x1, waiting for transfers between devices, on_device(): lax.all_to_all(carried, ('wide', 'narrow'), split_axis=2, concat_axis=1,...  24.5 us
    sub x8, matrix products, encoder_block(): shifted = jnp.exp(scores - jnp.max(scores, axis=-1, keepdims=True))  21.7 us
    dot_general x8, matrix products, encoder_block(): jnp.einsum('anhlm,amnhe->alnhe', weights, value_rows, preferred_element_t...  21.4 us
    dot_general x8, matrix products, encoder_block(): output = jnp.dot(hidden, down_weight, preferred_element_type=jnp.float32)  12.3 us
    dot_general x8, matrix products, encoder_block(): jnp.dot(attended, attn_weights[3], preferred_element_type=jnp.float32)  11.1 us
  transfers between devices with their start and end apart: 1, of which 1 were waited for; matrix products, arithmetic and copies ran while one was open for 0% of the time, Pallas kernels for 0%

commit v1 on v0

--- a/solution.py
+++ b/solution.py
@@ -118,7 +118,15 @@
         norm_bias,
         512,
     ).astype(jnp.bfloat16)
-    inter_out = lax.all_to_all(result, ("wide", "narrow"), split_axis=1, concat_axis=2, tiled=True)
+    inter_out = jnp.concatenate(
+        lax.all_to_all(
+            jnp.stack(jnp.split(result, lax.axis_size(("wide", "narrow")), axis=1)),
+            ("wide", "narrow"),
+            0,
+            0,
+        ),
+        axis=2,
+    )
     separated = group_norm(
         inter_out.astype(jnp.float32), group_gain[1], group_bias[1]
     ) + carried.astype(jnp.float32)

time: 290 us -> 316 us (1.090)
  local copies, waits for them, and re-layouts: 16.2 us -> 40.6 us
    unnamed x18 -> x49, local copies, waits for them, and re-layouts: 1.09 us -> 24.8 us
    another operation x24 -> x25, local copies, waits for them, and re-layouts: 6 us -> 6.76 us
where the time goes in v1:
time: 316 us; the launch traced here: 312 us
  blocking collectives  112 us (35%)
  matrix products  107 us (34%)
  local copies, waits for them, and re-layouts  40.6 us (13%)
  waiting for transfers between devices  24.5 us (8%)
  other arithmetic  22.1 us (7%)
  starting transfers between devices  3.87 us (1%)
    psum x2, blocking collectives, group_norm(): lax.psum((jnp.sum(values, axis=(1, 2, 3)), jnp.sum(values * values, axis=...  82.7 us
    all_to_all x1, blocking collectives, on_device(): lax.all_to_all(jnp.stack(jnp.split(result, lax.axis_size(('wide', 'narrow...  29.6 us
    dot_general x24, matrix products, project(): jnp.dot(normed, matrix, preferred_element_type=jnp.float32)  28.3 us
    unnamed x49, local copies, waits for them, and re-layouts  24.8 us
    all_to_all x1, waiting for transfers between devices, on_device(): lax.all_to_all(carried, ('wide', 'narrow'), split_axis=2, concat_axis=1,...  24.5 us
    sub x8, matrix products, encoder_block(): shifted = jnp.exp(scores - jnp.max(scores, axis=-1, keepdims=True))  21.7 us
    dot_general x8, matrix products, encoder_block(): jnp.einsum('anhlm,amnhe->alnhe', weights, value_rows, preferred_element_t...  21.4 us
    dot_general x8, matrix products, encoder_block(): output = jnp.dot(hidden, down_weight, preferred_element_type=jnp.float32)  12.2 us
  transfers between devices with their start and end apart: 1, of which 1 were waited for; matrix products, arithmetic and copies ran while one was open for 0% of the time, Pallas kernels for 0%

profile of v1, /device:TPU:10, one launch (start us, length us, event | category | flops | bytes accessed | tf_op | source)
XLA Modules:
  0.0 312.2 jit_solution(2540607632521563938)
XLA Ops:
  0.6 69.5 %while.20 = (s32[]{:T(128)}, f32[4,2,256,1,256]{4,2,1,3,0:T(8,128)S(1)}, bf16[4,2,256,1,256]{4,2,1,3,0:T(8,128)(2,1)}, f32[256,256]{1,0:T(8,128)S(1)}, f32[2,2,2...) while((s32[]{:T(128)}, ...), condition=%wide.region_7.8_spmd, body=%wide.region_0.7_spmd.sunk | while | flops 950011136 | bytes 32064172 | solution.py:79
  7.5 3.5 %fusion.222 = (f32[2,8,256]{2,1,0:T(8,128)S(1)}, f32[2,8,256,256]{2,3,1,0:T(8,128)}) fusion(bf16[2,256,8,32]{1,0,3,2:T(2,128)(2,1)S(1)} %reshape.947, bf16[2,256,8,32]{1,0,3,2:T(2,128)(2,1)S(1)} %reshape.948), kind=kOutput, calls=%fused_computation.214.clone.1 | convolution fusion | flops 70254848 | bytes 4734976 | tf_op jit(solution)/shard_map/while/body/eval_jaxpr/sub | solution.py:42
  12.4 2.6 fusion.223
  24.9 3.4 %fusion.222 = (f32[2,8,256]{2,1,0:T(8,128)S(1)}, f32[2,8,256,256]{2,3,1,0:T(8,128)}) fusion(bf16[2,256,8,32]{1,0,3,2:T(2,128)(2,1)S(1)} %reshape.947, bf16[2,256,8,32]{1,0,3,2:T(2,128)(2,1)S(1)} %reshape.948), kind=kOutput, calls=%fused_computation.214.clone.1 | convolution fusion | flops 70254848 | bytes 4734976 | tf_op jit(solution)/shard_map/while/body/eval_jaxpr/sub | solution.py:42
  29.7 2.6 fusion.223
  42.3 3.4 %fusion.222 = (f32[2,8,256]{2,1,0:T(8,128)S(1)}, f32[2,8,256,256]{2,3,1,0:T(8,128)}) fusion(bf16[2,256,8,32]{1,0,3,2:T(2,128)(2,1)S(1)} %reshape.947, bf16[2,256,8,32]{1,0,3,2:T(2,128)(2,1)S(1)} %reshape.948), kind=kOutput, calls=%fused_computation.214.clone.1 | convolution fusion | flops 70254848 | bytes 4734976 | tf_op jit(solution)/shard_map/while/body/eval_jaxpr/sub | solution.py:42
  47.1 2.6 fusion.223
  59.7 3.4 %fusion.222 = (f32[2,8,256]{2,1,0:T(8,128)S(1)}, f32[2,8,256,256]{2,3,1,0:T(8,128)}) fusion(bf16[2,256,8,32]{1,0,3,2:T(2,128)(2,1)S(1)} %reshape.947, bf16[2,256,8,32]{1,0,3,2:T(2,128)(2,1)S(1)} %reshape.948), kind=kOutput, calls=%fused_computation.214.clone.1 | convolution fusion | flops 70254848 | bytes 4734976 | tf_op jit(solution)/shard_map/while/body/eval_jaxpr/sub | solution.py:42
  64.5 2.6 fusion.223
  71.9 41.2 %all-reduce.1 = (f32[4]{0:T(128)S(1)}, f32[4]{0:T(128)S(1)}) all-reduce(f32[4]{0:T(128)S(1)} %fusion.125, f32[4]{0:T(128)S(1)} %reduce_sum.126), channel_id=1, replica_groups=mesh['wide'=4,'narrow'=8] {'wide','narrow'}, use_global_device_ids=true, to_apply=%region_11.12 | all-reduce | flops 8 | bytes 64 | tf_op jit(solution)/shard_map/psum | solution.py:86
  114.5 1.8 copy.85
  116.3 3.9 %all-to-all-start = ((bf16[4,2,256,256]{3,0,1,2:T(4,128)(2,1)}), bf16[4,2,256,256]{3,0,1,2:T(4,128)(2,1)S(1)}, u32[]{:S(2)}, u32[]{:S(2)}) async-start(bf16[4,2,256,256]{3,0,1,2:T(4,128)(2,1)} %copy.85), calls=%async_computation | async-start | bytes 2097152 | tf_op jit(solution)/shard_map/all_to_all | solution.py:112
  120.4 24.5 %all-to-all-done = bf16[4,2,256,256]{3,0,1,2:T(4,128)(2,1)S(1)} async-done(((bf16[4,2,256,256]{3,0,1,2:T(4,128)(2,1)}), bf16[4,2,256,256]{3,0,1,2:T(4,128)(2,1)S(1)}, u32[]{:S(2)}, u32[]{:S(2)}) %all-to-all-start) | async-done | bytes 1048608 | tf_op jit(solution)/shard_map/all_to_all | solution.py:112
  145.1 69.5 %while.21 = (s32[]{:T(128)}, bf16[4,1,64,8,256]{4,3,2,1,0:T(8,128)(2,1)}, bf16[4,1,64,8,256]{4,3,2,1,0:T(8,128)(2,1)S(1)}, f32[64,256]{1,0:T(8,128)S(1)}, f32[2,...) while((s32[]{:T(128)}, ...), condition=%wide.region_19.20_spmd, body=%wide.region_12.19_spmd.sunk | while | flops 864556160 | bytes 17468152 | solution.py:79
  148.9 2.7 fusion.246
  151.6 2.0 fusion.245
  155.3 2.7 convolution_convert_fusion.20
  159.8 2.6 fusion.248
  166.3 2.7 fusion.246
  169.0 2.0 fusion.245
  172.7 2.7 convolution_convert_fusion.20
  177.2 2.6 fusion.248
  183.7 2.7 fusion.246
  186.4 2.0 fusion.245
  190.0 2.7 convolution_convert_fusion.20
  194.6 2.6 fusion.248
  201.0 2.7 fusion.246
  203.7 2.0 fusion.245
  207.4 2.7 convolution_convert_fusion.20
  212.0 2.6 fusion.248
  239.0 29.6 %all_to_all.20 = bf16[32,4,2,8,256]{4,3,2,1,0:T(8,128)(2,1)S(1)} all-to-all(bf16[32,4,2,8,256]{4,3,2,1,0:T(8,128)(2,1)S(1)} %constant_dynamic-update-slice_fusion), channel_id=1, replica_groups=mesh['wide'=4,'narrow'=8] {'wide','narrow'}, dimensions={0} | all-to-all | bytes 2097152 | tf_op jit(solution)/shard_map/all_to_all | solution.py:122
  269.1 41.5 %all-reduce = (f32[4]{0:T(128)S(1)}, f32[4]{0:T(128)S(1)}) all-reduce(f32[4]{0:T(128)S(1)} %get-tuple-element.102, f32[4]{0:T(128)S(1)} %get-tuple-element.101), channel_id=1, replica_groups=mesh['wide'=4,'narrow'=8] {'wide','narrow'}, use_global_device_ids=true, to_apply=%region_23.24 | all-reduce | flops 8 | bytes 64 | tf_op jit(solution)/shard_map/psum | solution.py:86
  (275 shorter events, 103.9 us)
Async XLA Ops:
  15.0 2.1 copy-start.15
  15.0 2.5 copy-start.3
  32.3 2.1 copy-start.15
  32.4 2.5 copy-start.3
  49.7 2.1 copy-start.15
  49.7 2.5 copy-start.3
  67.1 2.1 copy-start.15
  67.1 2.5 copy-start.3
  70.1 43.0 %copy-start = (bf16[4,2,256,1,256]{4,2,1,3,0:T(8,128)(2,1)S(1)}, bf16[4,2,256,1,256]{4,2,1,3,0:T(8,128)(2,1)}, u32[]{:S(2)}) copy-start(bf16[4,2,256,1,256]{4,2,1,3,0:T(8,128)(2,1)} %get-tuple-element.371) | copy-start | bytes 3145732
  116.3 28.7 %copy-start.5 = (f32[2,2,256]{2,1,0:T(2,128)S(1)}, f32[2,2,256]{2,1,0:T(2,128)}, u32[]{:S(2)}) copy-start(f32[2,2,256]{2,1,0:T(2,128)} %get-tuple-element.375) | copy-start | bytes 12292
  116.3 28.7 %copy-start.6 = (f32[2,2,256]{2,1,0:T(2,128)S(1)}, f32[2,2,256]{2,1,0:T(2,128)}, u32[]{:S(2)}) copy-start(f32[2,2,256]{2,1,0:T(2,128)} %get-tuple-element.376) | copy-start | bytes 12292
  116.3 28.5 %all-to-all-start = ((bf16[4,2,256,256]{3,0,1,2:T(4,128)(2,1)}), bf16[4,2,256,256]{3,0,1,2:T(4,128)(2,1)S(1)}, u32[]{:S(2)}, u32[]{:S(2)}) async-start(bf16[4,2,256,256]{3,0,1,2:T(4,128)(2,1)} %copy.85), calls=%async_computation | async-start | bytes 2097152 | tf_op jit(solution)/shard_map/all_to_all | solution.py:112
  145.5 1.7 copy-start.7
  151.6 2.0 copy-start.8
  151.6 2.0 copy-start.10
  158.0 1.8 copy-start.4
  169.0 2.0 copy-start.8
  169.0 2.0 copy-start.10
  175.4 1.8 copy-start.4
  180.3 1.7 copy-start.7
  180.3 1.7 copy-start.9
  186.4 2.0 copy-start.8
  186.4 2.0 copy-start.10
  192.8 1.8 copy-start.4
  197.6 1.7 copy-start.7
  197.6 1.7 copy-start.9
  203.7 2.0 copy-start.8
  203.7 2.0 copy-start.10
  210.1 1.8 copy-start.4
  226.8 83.8 %copy-start.2 = (bf16[4,2,256,256]{3,2,1,0:T(8,128)(2,1)S(1)}, bf16[4,2,256,256]{3,2,1,0:T(8,128)(2,1)}, u32[]{:S(2)}) copy-start(bf16[4,2,256,256]{3,2,1,0:T(8,128)(2,1)} %copy-done.1) | copy-start | bytes 3145732
  226.8 83.8 %copy-start.11 = (f32[1,256]{1,0:T(1,128)S(1)}, f32[1,256]{1,0:T(1,128)}, u32[]{:S(2)}) copy-start(f32[1,256]{1,0:T(1,128)} %get-tuple-element.161) | copy-start | bytes 3076
  226.8 83.8 %copy-start.12 = (f32[1,256]{1,0:T(1,128)S(1)}, f32[1,256]{1,0:T(1,128)}, u32[]{:S(2)}) copy-start(f32[1,256]{1,0:T(1,128)} %get-tuple-element.163) | copy-start | bytes 3076
  (6 other events, 8.0 us)
